TPU v7x, 32 devices: a whole 2x2x4 slice. The times are simulated.
32 devices in a mesh: aa: 2 (over core), ba: 16 (over z, y, x).
Axes of the slice: x: 2, y: 2, z: 4, core: 2. Of those that a mesh axis runs over, the one named last changes fastest.
Arguments:
- queries: bfloat16 [2, 16, 192, 1024], P('aa', 'ba'), may hold values from -6 to 6
- key_rows: bfloat16 [2, 16, 192, 1024], P('aa', 'ba'), may hold values from -6 to 6
- value_rows: bfloat16 [2, 16, 192, 1024], P('aa', 'ba'), may hold values from -6 to 6
- out_proj: bfloat16 [2, 1024, 1024], P('aa', 'ba'), may hold values from -0.1875 to 0.1875
- scale_ids: int32 [16, 192], P('ba'), may hold values from 0 to 7, never falling along the last dimension, each value on 1 to 64 neighbouring positions
- residual_in: bfloat16 [16, 192, 1024], P('ba'), may hold values from -4 to 4
- cotangent: bfloat16 [16, 192, 1024], P('ba'), may hold values from -6 to 6
Outputs:
- residual_out: bfloat16 [2, 16, 192, 1024], P('aa', 'ba')
- grad_query: bfloat16 [2, 16, 192, 1024], P('aa', 'ba')
- grad_key: bfloat16 [2, 16, 192, 1024], P('aa', 'ba')
- grad_value: bfloat16 [2, 16, 192, 1024], P('aa', 'ba')
- grad_proj: float32 [2, 1024, 1024], P('aa', 'ba')
Inputs may be any that keep to these rules, and one draw needn't show every extreme that they name: `scale_ids`: for each image the scale ids never fall along the tokens; every scale from 0 to 7 is present, with 1 to 64 tokens.
All inputs are finite; a program needn't handle non-finite values.
Results may differ from a plain program's by a relative error of at most 0.0086.
Values may be sent and summed in bfloat16 or wider, within the bound.
No kernel may reach another device: no remote copies, remote signals or barrier semaphores. Data moves between devices by JAX's collectives and lax.ppermute only.
A program may use at most 64 MiB of HBM per device.

v0:
```python
import jax
import jax.numpy as jnp
from jax import lax
from jax.sharding import PartitionSpec as P

HD = 64


def passed_along(value, axis, by):
    devices = lax.axis_size(axis)
    pairs = [(i, i + by) for i in range(devices) if 0 <= i + by < devices]
    return lax.ppermute(value, axis, pairs)


def local(queries, key_rows, value_rows, out_proj, scale_ids, residual_in, cotangent):
    images = queries.shape[1]
    length = queries.shape[2]
    inner_width = queries.shape[3]
    head_count = inner_width // HD
    res_width = residual_in.shape[2]
    flat_rows = images * length
    score_scale = HD ** (-0.5)
    image_weight = 1.0 / (lax.axis_size("ba") * images)
    w_full = lax.all_gather(out_proj, "ba", axis=1, tiled=True)[0]
    visible = scale_ids[:, None, :] <= scale_ids[:, :, None]
    q_heads = queries[0].reshape(images, length, head_count, HD)
    k_heads = key_rows[0].reshape(images, length, head_count, HD)
    v_heads = value_rows[0].reshape(images, length, head_count, HD)
    scores = (
        jnp.einsum("bihd,bjhd->bhij", q_heads, k_heads, preferred_element_type=jnp.float32)
        * score_scale
    )
    scores = jnp.where(visible[:, None], scores, -jnp.inf)
    row_max = jnp.max(scores, axis=-1, keepdims=True)
    lifted = jnp.exp(scores - row_max)
    attn_probs = lifted / jnp.sum(lifted, axis=-1, keepdims=True)
    probs_low = attn_probs.astype(jnp.bfloat16)
    attended = jnp.einsum("bhij,bjhd->bihd", probs_low, v_heads, preferred_element_type=jnp.float32)
    attn_rows = attended.astype(jnp.bfloat16).reshape(flat_rows, inner_width)
    branch = jnp.dot(attn_rows, w_full, preferred_element_type=jnp.float32)

    def relay_step(hop_index, running):
        return branch + passed_along(running, "aa", 1)

    carried = lax.fori_loop(0, lax.axis_size("aa") - 1, relay_step, branch)
    residual_rows = residual_in.reshape(flat_rows, res_width).astype(jnp.float32) + carried
    residual_out = residual_rows.astype(jnp.bfloat16).reshape(images, length, res_width)
    cot_rows = cotangent.reshape(flat_rows, res_width)
    d_attn = lax.dot_general(
        cot_rows, w_full, (((1,), (1,)), ((), ())), preferred_element_type=jnp.float32
    ).astype(jnp.bfloat16)
    product = lax.dot_general(
        attn_rows, cot_rows, (((0,), (0,)), ((), ())), preferred_element_type=jnp.float32
    )
    grad_proj = lax.psum_scatter(product * image_weight, "ba", scatter_dimension=0, tiled=True)
    d_heads = d_attn.reshape(images, length, head_count, HD)
    grad_value = jnp.einsum(
        "bhij,bihd->bjhd", probs_low, d_heads, preferred_element_type=jnp.float32
    )
    d_probs = jnp.einsum("bihd,bjhd->bhij", d_heads, v_heads, preferred_element_type=jnp.float32)
    row_delta = jnp.sum(attn_probs * d_probs, axis=-1, keepdims=True)
    d_scores = (attn_probs * (d_probs - row_delta) * score_scale).astype(jnp.bfloat16)
    grad_query = jnp.einsum(
        "bhij,bjhd->bihd", d_scores, k_heads, preferred_element_type=jnp.float32
    )
    grad_key = jnp.einsum("bhij,bihd->bjhd", d_scores, q_heads, preferred_element_type=jnp.float32)
    return (
        residual_out[None],
        grad_query.reshape(images, length, inner_width).astype(jnp.bfloat16)[None],
        grad_key.reshape(images, length, inner_width).astype(jnp.bfloat16)[None],
        grad_value.reshape(images, length, inner_width).astype(jnp.bfloat16)[None],
        grad_proj[None],
    )


def solution(mesh):
    placed = (
        P("aa", "ba", None, None),
        P("aa", "ba", None, None),
        P("aa", "ba", None, None),
        P("aa", "ba", None),
        P("ba", None),
        P("ba", None, None),
        P("ba", None, None),
    )
    return jax.shard_map(
        local,
        mesh=mesh,
        in_specs=placed,
        out_specs=(
            P("aa", "ba", None, None),
            P("aa", "ba", None, None),
            P("aa", "ba", None, None),
            P("aa", "ba", None, None),
            P("aa", "ba", None),
        ),
        check_vma=False,
    )
```

profile of v0, /device:TPU:0, one launch (start us, length us, event | category | flops | bytes accessed | tf_op | source)
XLA Modules:
  0.0 177.7 jit_solution(12900894556805366626)
XLA Ops:
  7.2 0.0 copy-start
  7.2 0.0 all-gather.2.cloned.1.call-start
  7.2 0.7 all-gather.2.cloned.1.call-update
  7.9 0.0 reduce-scatter.2.cloned.1.call-start
  8.0 1.2 copy.27
  9.2 0.0 copy-start.4
  9.2 1.4 copy.28
  10.6 0.0 copy-start.2
  10.6 1.4 copy.29
  12.0 0.8 broadcast_compare_fusion
  12.8 2.9 %fusion.44 = (f32[16,192]{1,0:T(8,128)S(1)}, f32[16,192,192]{1,2,0:T(8,128)}) fusion(pred[192,192]{0,1:T(8,128)(4,1)S(1)} %broadcast_compare_fusion, bf16[192,16,64]{0,2,1:T(8,128)(2,1)S(1)} %bitcast.69, bf16[192,16,64]{0,2,1:T(8,128)(2,1)S(1)} %bitcast.67), kind=kOutput, calls=%fused_computation.41 | convolution fusion | flops 77856960 | bytes 3194880 | tf_op jit(solution)/shard_map/sub | solution.py:35
  15.8 0.0 copy-done.4
  15.8 2.3 %convolution_convert_fusion = bf16[16,192,64]{1,2,0:T(8,128)(2,1)S(1)} fusion(bf16[192,16,64]{0,2,1:T(8,128)(2,1)S(1)} %bitcast.63, f32[16,192,192]{1,2,0:T(8,128)} %get-tuple-element.25, f32[16,192]{1,0:T(8,128)S(1)} %get-tuple-element.24), kind=kOutput, calls=%fused_computation.23 | convolution fusion | flops 76873728 | bytes 3158016 | tf_op jit(solution)/shard_map/bhij,bjhd->bihd/dot_general | solution.py:38
  18.1 2.6 %convolution_multiply_fusion = f32[1024,1024]{1,0:T(8,128)} fusion(bf16[192,1024]{0,1:T(8,128)(2,1)S(1)} %bitcast.61, bf16[1,192,1024]{2,1,0:T(8,128)(2,1)S(1)} %copy-done), kind=kOutput, calls=%fused_computation.8 | convolution fusion | flops 403701760 | bytes 4980736 | tf_op jit(solution)/shard_map/dot_general | solution.py:52
  20.7 0.0 reduce-scatter.2.cloned.1.call-update
  20.8 53.1 %all-gather.2.cloned.1.call-done = bf16[1,1024,1024]{2,1,0:T(8,128)(2,1)} async-done(((bf16[1,64,1024]{2,1,0:T(8,128)(2,1)}), bf16[1,1024,1024]{2,1,0:T(8,128)(2,1)}) %all-gather.2.cloned.1.call-update) | async-done | bytes 2097168 | tf_op jit(solution)/shard_map/all_gather | solution.py:24
  73.9 2.3 %fusion.8 = f32[192,1024]{1,0:T(8,128)S(1)} fusion(bf16[192,1024]{0,1:T(8,128)(2,1)S(1)} %bitcast.62, bf16[1,1024,1024]{2,1,0:T(8,128)(2,1)} %all-gather.2.cloned.1.call-done), kind=kOutput, calls=%fused_computation.11 | convolution fusion | flops 402653184 | bytes 3276800 | tf_op jit(solution)/shard_map/dot_general | solution.py:40
  76.2 1.3 collective-permute-start
  77.6 0.0 copy-done.1
  77.6 0.9 fusion.27
  78.5 0.2 copy.31
  78.7 2.3 %fusion.45 = f32[16,192,192]{1,2,0:T(8,128)} fusion(bf16[192,16,64]{0,2,1:T(8,128)(2,1)S(1)} %bitcast.65, bf16[192,16,64]{0,2,1:T(8,128)(2,1)S(1)} %bitcast.64), kind=kOutput, calls=%fused_computation.42 | convolution fusion | flops 75497472 | bytes 3145728 | tf_op jit(solution)/shard_map/bihd,bjhd->bhij/dot_general | solution.py:60
  81.0 0.0 copy-done.5
  81.0 6.6 %fusion.24 = bf16[16,192,64]{1,2,0:T(8,128)(2,1)} fusion(bf16[192,16,64]{0,2,1:T(8,128)(2,1)S(1)} %bitcast.70, f32[16,192,192]{1,2,0:T(8,128)} %fusion.45, f32[16,192,192]{1,2,0:T(8,128)} %get-tuple-element.25, f32[16,192]{1,0:T(8,128)S(1)} %get-tuple-element.24), kind=kOutput, calls=%fused_computation.22 | convolution fusion | flops 79826112 | bytes 5517312 | tf_op jit(solution)/shard_map/bhij,bihd->bjhd/dot_general | solution.py:66
  87.7 2.0 %copy.36 = bf16[1,1,192,1024]{3,2,1,0:T(8,128)(2,1)} copy(bf16[1,1,192,1024]{2,3,1,0:T(8,128)(2,1)} %bitcast.73) | data formatting | bytes 786432
  89.6 5.8 %fusion.21 = bf16[16,192,64]{1,2,0:T(8,128)(2,1)S(1)} fusion(bf16[192,16,64]{0,2,1:T(8,128)(2,1)S(1)} %bitcast.68, f32[16,192,192]{1,2,0:T(8,128)} %fusion.45, f32[16,192,192]{1,2,0:T(8,128)} %get-tuple-element.25, f32[16,192]{1,0:T(8,128)S(1)} %get-tuple-element.24), kind=kOutput, calls=%fused_computation.21 | convolution fusion | flops 79826112 | bytes 5517312 | tf_op jit(solution)/shard_map/bhij,bjhd->bihd/dot_general | solution.py:63
  95.5 0.9 copy.35
  96.4 2.6 %convolution_convert_fusion.1 = bf16[16,64,192]{2,1,0:T(8,128)(2,1)S(1)} fusion(bf16[192,16,64]{0,2,1:T(8,128)(2,1)S(1)} %bitcast.66, f32[16,192,192]{1,2,0:T(8,128)} %get-tuple-element.25, f32[16,192]{1,0:T(8,128)S(1)} %get-tuple-element.24), kind=kOutput, calls=%fused_computation.24 | convolution fusion | flops 76873728 | bytes 3158016 | tf_op jit(solution)/shard_map/bhij,bihd->bjhd/dot_general | solution.py:57
  99.0 0.9 copy.37
  99.9 0.0 collective-permute-done
  99.9 0.9 fusion.33
  100.9 69.9 %reduce-scatter.2.cloned.1.call-done = f32[64,1024]{1,0:T(8,128)} async-done(((f32[1024,1024]{1,0:T(8,128)}), f32[64,1024]{1,0:T(8,128)}) %reduce-scatter.2.cloned.1.call-update) | async-done | bytes 262160 | tf_op jit(solution)/shard_map/reduce_scatter | solution.py:55
  (8 shorter events, 0.0 us)
Async XLA Ops:
  7.2 10.9 %copy-start = (bf16[1,192,1024]{2,1,0:T(8,128)(2,1)S(1)}, bf16[1,192,1024]{2,1,0:T(8,128)(2,1)}, u32[]{:S(2)}) copy-start(bf16[1,192,1024]{2,1,0:T(8,128)(2,1)} %param.13) | copy-start | bytes 1179652
  7.2 66.7 %all-gather.2.cloned.1.call-start = ((), (), s32[]{:S(2)}) async-start(), calls=%async_computation.1 | async-start | bytes 2228224 | tf_op jit(solution)/shard_map/all_gather | solution.py:24
  7.9 162.9 %reduce-scatter.2.cloned.1.call-start = ((), (), s32[]{:S(2)}) async-start(), calls=%async_computation.2 | async-start | bytes 4456448 | tf_op jit(solution)/shard_map/reduce_scatter | solution.py:55
  9.2 6.6 %copy-start.4 = (bf16[1,1,192,1024]{2,3,1,0:T(8,128)(2,1)}, bf16[1,1,192,1024]{2,3,1,0:T(8,128)(2,1)S(1)}, u32[]{:S(2)}) copy-start(bf16[1,1,192,1024]{2,3,1,0:T(8,128)(2,1)S(1)} %copy.27) | copy-start | bytes 1179652
  10.6 5.2 %copy-start.2 = (bf16[1,1,192,1024]{2,3,1,0:T(8,128)(2,1)}, bf16[1,1,192,1024]{2,3,1,0:T(8,128)(2,1)S(1)}, u32[]{:S(2)}) copy-start(bf16[1,1,192,1024]{2,3,1,0:T(8,128)(2,1)S(1)} %copy.28) | copy-start | bytes 1179652
  73.9 3.7 %copy-start.1 = (bf16[1,1024,1024]{2,1,0:T(8,128)(2,1)S(1)}, bf16[1,1024,1024]{2,1,0:T(8,128)(2,1)}, u32[]{:S(2)}) copy-start(bf16[1,1024,1024]{2,1,0:T(8,128)(2,1)} %all-gather.2.cloned.1.call-done) | copy-start | bytes 6291460
  76.2 23.7 %collective-permute-start = (f32[192,1024]{1,0:T(8,128)S(1)}, f32[192,1024]{1,0:T(8,128)S(1)}, u32[]{:S(2)}, u32[]{:S(2)}) collective-permute-start(f32[192,1024]{1,0:T(8,128)S(1)} %fusion.8), channel_id=1, source_target_pairs={{0,16},{1,17},{2,18},{3,19},{4,20},{5,21},{6,22},{7,23},{8,24},{9,... | collective-permute-start | bytes 2359304 | tf_op jit(solution)/shard_map/while/body/eval_jaxpr/ppermute | solution.py:12
  78.7 2.4 %copy-start.5 = (bf16[1,1,192,1024]{2,3,1,0:T(8,128)(2,1)S(1)}, bf16[1,1,192,1024]{2,3,1,0:T(8,128)(2,1)}, u32[]{:S(2)}) copy-start(bf16[1,1,192,1024]{2,3,1,0:T(8,128)(2,1)} %copy-done.4) | copy-start | bytes 1179652
  81.0 8.6 %copy-start.3 = (bf16[1,1,192,1024]{2,3,1,0:T(8,128)(2,1)S(1)}, bf16[1,1,192,1024]{2,3,1,0:T(8,128)(2,1)}, u32[]{:S(2)}) copy-start(bf16[1,1,192,1024]{2,3,1,0:T(8,128)(2,1)} %copy-done.2) | copy-start | bytes 1179652
  96.4 3.5 %copy-start.6 = (bf16[1,192,1024]{2,1,0:T(8,128)(2,1)S(1)}, bf16[1,192,1024]{2,1,0:T(8,128)(2,1)}, u32[]{:S(2)}) copy-start(bf16[1,192,1024]{2,1,0:T(8,128)(2,1)} %param.12) | copy-start | bytes 1179652
Sparse Core Ops, SparseCore 0:
  10.8 63.0 all-gather.1
  76.8 94.0 reduce-scatter.1
where the time goes:
time: 178 us
  waiting for transfers between devices  124 us (70%)
  matrix products  28.5 us (16%)
  between operations  14.2 us (8%)
  local copies, waits for them, and re-layouts  8.07 us (5%)
  other arithmetic  1.78 us (1%)
    reduce_scatter x1, waiting for transfers between devices, local(): lax.psum_scatter(product * image_weight, 'ba', scatter_dimension=0, tiled...  69.9 us
    all_gather x1, waiting for transfers between devices, local(): w_full = lax.all_gather(out_proj, 'ba', axis=1, tiled=True)[0]  53.1 us
    unnamed x20, local copies, waits for them, and re-layouts  7.87 us
    dot_general x1, matrix products, local(): jnp.einsum('bhij,bihd->bjhd', d_scores, q_heads, preferred_element_type=j...  6.62 us
    dot_general x1, matrix products, local(): jnp.einsum('bhij,bjhd->bihd', d_scores, k_heads, preferred_element_type=j...  5.82 us
  transfers between devices with their start and end apart: 3, of which 2 were waited for; matrix products, arithmetic and copies ran while one was open for 22% of the time, Pallas kernels for 0%

commit v1 on v0

--- a/solution.py
+++ b/solution.py
@@ -21,7 +21,10 @@
     flat_rows = images * length
     score_scale = HD ** (-0.5)
     image_weight = 1.0 / (lax.axis_size("ba") * images)
-    w_full = lax.all_gather(out_proj, "ba", axis=1, tiled=True)[0]
+    _step_on_routes_all = lambda base_x, named_axis: jnp.concatenate(
+        lax.all_gather(base_x, named_axis), 1
+    )
+    w_full = _step_on_routes_all(out_proj, "ba")[0]
     visible = scale_ids[:, None, :] <= scale_ids[:, :, None]
     q_heads = queries[0].reshape(images, length, head_count, HD)
     k_heads = key_rows[0].reshape(images, length, head_count, HD)

time: 178 us -> 178 us (level)
  no operation moved by 1% of the time
where the time goes in v1:
time: 178 us
  waiting for transfers between devices  124 us (70%)
  matrix products  28.5 us (16%)
  between operations  14.2 us (8%)
  local copies, waits for them, and re-layouts  8.07 us (5%)
  other arithmetic  1.78 us (1%)
    reduce_scatter x1, waiting for transfers between devices, local(): lax.psum_scatter(product * image_weight, 'ba', scatter_dimension=0, tiled...  69.9 us
    all_gather x1, waiting for transfers between devices, local(): lax.all_gather(base_x, named_axis)  53.1 us
    unnamed x20, local copies, waits for them, and re-layouts  7.87 us
    dot_general x1, matrix products, local(): jnp.einsum('bhij,bihd->bjhd', d_scores, q_heads, preferred_element_type=j...  6.62 us
    dot_general x1, matrix products, local(): jnp.einsum('bhij,bjhd->bihd', d_scores, k_heads, preferred_element_type=j...  5.82 us
  transfers between devices with their start and end apart: 3, of which 2 were waited for; matrix products, arithmetic and copies ran while one was open for 22% of the time, Pallas kernels for 0%

profile of v1, /device:TPU:0, one launch (start us, length us, event | category | flops | bytes accessed | tf_op | source)
XLA Modules:
  0.0 177.7 jit_solution(5062084728257037514)
XLA Ops:
  7.2 0.0 copy-start
  7.2 0.0 all-gather.3.cloned.1.call-start
  7.2 0.7 all-gather.3.cloned.1.call-update
  7.9 0.0 reduce-scatter.2.cloned.1.call-start
  8.0 1.2 copy.38
  9.2 0.0 copy-start.4
  9.2 1.4 copy.39
  10.6 0.0 copy-start.2
  10.6 1.4 copy.40
  12.0 0.8 broadcast_compare_fusion
  12.8 2.9 %fusion.37 = (f32[16,192]{1,0:T(8,128)S(1)}, f32[16,192,192]{1,2,0:T(8,128)}) fusion(pred[192,192]{0,1:T(8,128)(4,1)S(1)} %broadcast_compare_fusion, bf16[192,16,64]{0,2,1:T(8,128)(2,1)S(1)} %bitcast.67, bf16[192,16,64]{0,2,1:T(8,128)(2,1)S(1)} %bitcast.65), kind=kOutput, calls=%fused_computation.37 | convolution fusion | flops 77856960 | bytes 3194880 | tf_op jit(solution)/shard_map/sub | solution.py:38
  15.8 0.0 copy-done.4
  15.8 2.3 %convolution_convert_fusion = bf16[16,192,64]{1,2,0:T(8,128)(2,1)S(1)} fusion(bf16[192,16,64]{0,2,1:T(8,128)(2,1)S(1)} %bitcast.61, f32[16,192,192]{1,2,0:T(8,128)} %get-tuple-element.30, f32[16,192]{1,0:T(8,128)S(1)} %get-tuple-element.29), kind=kOutput, calls=%fused_computation.19 | convolution fusion | flops 76873728 | bytes 3158016 | tf_op jit(solution)/shard_map/bhij,bjhd->bihd/dot_general | solution.py:41
  18.1 2.6 %convolution_multiply_fusion = f32[1024,1024]{1,0:T(8,128)} fusion(bf16[192,1024]{0,1:T(8,128)(2,1)S(1)} %bitcast.59, bf16[1,192,1024]{2,1,0:T(8,128)(2,1)S(1)} %copy-done), kind=kOutput, calls=%fused_computation.8 | convolution fusion | flops 403701760 | bytes 4980736 | tf_op jit(solution)/shard_map/dot_general | solution.py:55
  20.7 0.0 reduce-scatter.2.cloned.1.call-update
  20.8 53.1 %all-gather.3.cloned.1.call-done = bf16[16,64,1024]{2,1,0:T(8,128)(2,1)} async-done(((bf16[1,64,1024]{2,1,0:T(8,128)(2,1)}), bf16[16,64,1024]{2,1,0:T(8,128)(2,1)}) %all-gather.3.cloned.1.call-update) | async-done | bytes 2097168 | tf_op jit(solution)/shard_map/all_gather | solution.py:25
  73.9 2.3 %fusion.38 = f32[192,1024]{1,0:T(8,128)S(1)} fusion(bf16[192,1024]{0,1:T(8,128)(2,1)S(1)} %bitcast.60, bf16[1024,1024]{1,0:T(8,128)(2,1)} %bitcast.57), kind=kOutput, calls=%fused_computation.38 | convolution fusion | flops 402653184 | bytes 3276800 | tf_op jit(solution)/shard_map/dot_general | solution.py:43
  76.2 1.3 collective-permute-start
  77.6 0.0 copy-done.1
  77.6 0.9 convolution_convert_fusion.2
  78.5 0.2 copy.42
  78.7 2.3 %fusion.39 = f32[16,192,192]{1,2,0:T(8,128)} fusion(bf16[192,16,64]{0,2,1:T(8,128)(2,1)S(1)} %bitcast.63, bf16[192,16,64]{0,2,1:T(8,128)(2,1)S(1)} %bitcast.62), kind=kOutput, calls=%fused_computation.39 | convolution fusion | flops 75497472 | bytes 3145728 | tf_op jit(solution)/shard_map/bihd,bjhd->bhij/dot_general | solution.py:63
  81.0 0.0 copy-done.5
  81.0 6.6 %fusion.20 = bf16[16,192,64]{1,2,0:T(8,128)(2,1)} fusion(bf16[192,16,64]{0,2,1:T(8,128)(2,1)S(1)} %bitcast.68, f32[16,192,192]{1,2,0:T(8,128)} %fusion.39, f32[16,192,192]{1,2,0:T(8,128)} %get-tuple-element.30, f32[16,192]{1,0:T(8,128)S(1)} %get-tuple-element.29), kind=kOutput, calls=%fused_computation.18 | convolution fusion | flops 79826112 | bytes 5517312 | tf_op jit(solution)/shard_map/bhij,bihd->bjhd/dot_general | solution.py:69
  87.7 2.0 %copy.47 = bf16[1,1,192,1024]{3,2,1,0:T(8,128)(2,1)} copy(bf16[1,1,192,1024]{2,3,1,0:T(8,128)(2,1)} %bitcast.71) | data formatting | bytes 786432
  89.6 5.8 %fusion.17 = bf16[16,192,64]{1,2,0:T(8,128)(2,1)S(1)} fusion(bf16[192,16,64]{0,2,1:T(8,128)(2,1)S(1)} %bitcast.66, f32[16,192,192]{1,2,0:T(8,128)} %fusion.39, f32[16,192,192]{1,2,0:T(8,128)} %get-tuple-element.30, f32[16,192]{1,0:T(8,128)S(1)} %get-tuple-element.29), kind=kOutput, calls=%fused_computation.17 | convolution fusion | flops 79826112 | bytes 5517312 | tf_op jit(solution)/shard_map/bhij,bjhd->bihd/dot_general | solution.py:66
  95.5 0.9 copy.46
  96.4 2.6 %convolution_convert_fusion.1 = bf16[16,64,192]{2,1,0:T(8,128)(2,1)S(1)} fusion(bf16[192,16,64]{0,2,1:T(8,128)(2,1)S(1)} %bitcast.64, f32[16,192,192]{1,2,0:T(8,128)} %get-tuple-element.30, f32[16,192]{1,0:T(8,128)S(1)} %get-tuple-element.29), kind=kOutput, calls=%fused_computation.20 | convolution fusion | flops 76873728 | bytes 3158016 | tf_op jit(solution)/shard_map/bhij,bihd->bjhd/dot_general | solution.py:60
  99.0 0.9 copy.48
  99.9 0.0 collective-permute-done
  99.9 0.9 fusion.26
  100.9 69.9 %reduce-scatter.2.cloned.1.call-done = f32[64,1024]{1,0:T(8,128)} async-done(((f32[1024,1024]{1,0:T(8,128)}), f32[64,1024]{1,0:T(8,128)}) %reduce-scatter.2.cloned.1.call-update) | async-done | bytes 262160 | tf_op jit(solution)/shard_map/reduce_scatter | solution.py:58
  (8 shorter events, 0.0 us)
Async XLA Ops:
  7.2 10.9 %copy-start = (bf16[1,192,1024]{2,1,0:T(8,128)(2,1)S(1)}, bf16[1,192,1024]{2,1,0:T(8,128)(2,1)}, u32[]{:S(2)}) copy-start(bf16[1,192,1024]{2,1,0:T(8,128)(2,1)} %param.13) | copy-start | bytes 1179652
  7.2 66.7 %all-gather.3.cloned.1.call-start = ((), (), s32[]{:S(2)}) async-start(), calls=%async_computation.2 | async-start | bytes 2228224 | tf_op jit(solution)/shard_map/all_gather | solution.py:25
  7.9 162.9 %reduce-scatter.2.cloned.1.call-start = ((), (), s32[]{:S(2)}) async-start(), calls=%async_computation.1 | async-start | bytes 4456448 | tf_op jit(solution)/shard_map/reduce_scatter | solution.py:58
  9.2 6.6 %copy-start.4 = (bf16[1,1,192,1024]{2,3,1,0:T(8,128)(2,1)}, bf16[1,1,192,1024]{2,3,1,0:T(8,128)(2,1)S(1)}, u32[]{:S(2)}) copy-start(bf16[1,1,192,1024]{2,3,1,0:T(8,128)(2,1)S(1)} %copy.38) | copy-start | bytes 1179652
  10.6 5.2 %copy-start.2 = (bf16[1,1,192,1024]{2,3,1,0:T(8,128)(2,1)}, bf16[1,1,192,1024]{2,3,1,0:T(8,128)(2,1)S(1)}, u32[]{:S(2)}) copy-start(bf16[1,1,192,1024]{2,3,1,0:T(8,128)(2,1)S(1)} %copy.39) | copy-start | bytes 1179652
  73.9 3.7 %copy-start.1 = (bf16[16,64,1024]{2,1,0:T(8,128)(2,1)S(1)}, bf16[16,64,1024]{2,1,0:T(8,128)(2,1)}, u32[]{:S(2)}) copy-start(bf16[16,64,1024]{2,1,0:T(8,128)(2,1)} %all-gather.3.cloned.1.call-done) | copy-start | bytes 6291460
  76.2 23.7 %collective-permute-start = (f32[192,1024]{1,0:T(8,128)S(1)}, f32[192,1024]{1,0:T(8,128)S(1)}, u32[]{:S(2)}, u32[]{:S(2)}) collective-permute-start(f32[192,1024]{1,0:T(8,128)S(1)} %fusion.38), channel_id=1, source_target_pairs={{0,16},{1,17},{2,18},{3,19},{4,20},{5,21},{6,22},{7,23},{8,24},{9,... | collective-permute-start | bytes 2359304 | tf_op jit(solution)/shard_map/while/body/eval_jaxpr/ppermute | solution.py:12
  78.7 2.4 %copy-start.5 = (bf16[1,1,192,1024]{2,3,1,0:T(8,128)(2,1)S(1)}, bf16[1,1,192,1024]{2,3,1,0:T(8,128)(2,1)}, u32[]{:S(2)}) copy-start(bf16[1,1,192,1024]{2,3,1,0:T(8,128)(2,1)} %copy-done.4) | copy-start | bytes 1179652
  81.0 8.6 %copy-start.3 = (bf16[1,1,192,1024]{2,3,1,0:T(8,128)(2,1)S(1)}, bf16[1,1,192,1024]{2,3,1,0:T(8,128)(2,1)}, u32[]{:S(2)}) copy-start(bf16[1,1,192,1024]{2,3,1,0:T(8,128)(2,1)} %copy-done.2) | copy-start | bytes 1179652
  96.4 3.5 %copy-start.6 = (bf16[1,192,1024]{2,1,0:T(8,128)(2,1)S(1)}, bf16[1,192,1024]{2,1,0:T(8,128)(2,1)}, u32[]{:S(2)}) copy-start(bf16[1,192,1024]{2,1,0:T(8,128)(2,1)} %param.12) | copy-start | bytes 1179652
Sparse Core Ops, SparseCore 0:
  10.8 63.0 all-gather.2
  76.8 94.0 reduce-scatter.1
